TPU v7x, 32 devices: a whole 2x2x4 slice. The times are simulated.
32 devices in a mesh: segment: 4 (over y, core), shard: 8 (over z, x).
Axes of the slice: x: 2, y: 2, z: 4, core: 2. Of those that a mesh axis runs over, the one named last changes fastest.
Arguments:
- buffer: bfloat16 [8, 18432, 2304], P('segment', 'shard'), may hold values from -6 to 6
- right_basis: bfloat16 [8, 2304, 256], P('segment', 'shard'), may hold values from -0.125 to 0.125
- layer_count: int32 [4], P('segment'), may hold values from 1 to 2, as said below
Outputs:
- momentum_out: bfloat16 [8, 18432, 2304], P('segment', 'shard')
- left_step: bfloat16 [8, 18432, 256], P('segment', 'shard')
- right_step: float32 [8, 2304, 256], P('segment', 'shard')
Inputs may be any that keep to these rules, and one draw needn't show every extreme that they name: `layer_count`: each segment uses between 1 and 2 slots; some segment uses 2 and some segment uses 1.
All inputs are finite; a program needn't handle non-finite values.
Results may differ from a plain program's by a relative error of at most 0.0024.
Values may be sent and summed in bfloat16 or wider, within the bound.
A program may use at most 128 MiB of HBM per device.

v0:
```python
import math
import jax
import jax.numpy as jnp
from jax import lax
from jax.sharding import PartitionSpec as P

MOMENTUM = 0.9
CLIP_RMS = 0.35
SQUARE_FLOOR = 0.0625


def finish_basis(proj, gram):
    lower = jnp.linalg.cholesky(gram)
    solved = jax.scipy.linalg.solve_triangular(lower, jnp.swapaxes(proj, 1, 2), lower=True)
    return jnp.swapaxes(solved, 1, 2)


def right_factor(partial_value):
    groups = lax.axis_size("shard")
    cols = partial_value.shape[1]
    width = cols // groups
    full = lax.psum(partial_value, "shard")
    colsq = jnp.sum(full * full, axis=1, keepdims=True)
    scaled = full * (math.sqrt(cols) * lax.rsqrt(colsq + 1.0))
    local = lax.dynamic_slice_in_dim(scaled, lax.axis_index("shard") * width, width, 1)
    return (full.astype(jnp.bfloat16), local)


def finish_layers(block, proj, gram, used, clip, rows_all):
    ortho = finish_basis(proj, gram)
    half_left = ortho.astype(jnp.bfloat16)
    partial_value = jnp.einsum("kij,kir->kjr", block, half_left, preferred_element_type=jnp.float32)
    half_right, right_local = right_factor(partial_value)
    correction = jnp.einsum(
        "kir,kjr->kij", half_left, half_right, preferred_element_type=jnp.float32
    )
    keep = used[:, None, None]
    moment = jnp.where(keep, block - (1.0 - MOMENTUM) * correction, 0.0).astype(jnp.bfloat16)
    left = jnp.where(keep, clip * math.sqrt(rows_all) * ortho, 0.0).astype(jnp.bfloat16)
    right = jnp.where(keep, right_local, 0.0)
    return (moment, left, right)


def body(buffer, right_basis, layer_count):
    slots = buffer.shape[0]
    rows_dev = buffer.shape[1]
    cols = buffer.shape[2]
    rows_all = rows_dev * lax.axis_size("shard")
    count = layer_count[0]
    used = jnp.arange(slots, dtype=jnp.int32) < count
    per_slot = jnp.sum(jnp.square(buffer.astype(jnp.float32)), axis=(1, 2))
    local_sq = jnp.sum(jnp.where(used, per_slot, 0.0))
    local_elems = count.astype(jnp.float32) * float(rows_dev * cols)
    total_sq, total_elems = lax.psum((local_sq, local_elems), ("segment", "shard"))
    clip = jnp.minimum(1.0, CLIP_RMS * lax.rsqrt(jnp.maximum(total_sq / total_elems, SQUARE_FLOOR)))
    proj = jnp.einsum(
        "kij,kjr->kir",
        buffer,
        lax.all_gather(right_basis, "shard", axis=1, tiled=True),
        preferred_element_type=jnp.float32,
    )
    local_gram = jnp.einsum("kir,kis->krs", proj, proj, precision=lax.Precision.HIGHEST)
    gram = lax.psum(local_gram, "shard")
    return finish_layers(buffer, proj, gram, used, clip, rows_all)


def solution(mesh):
    in_specs = (P("segment", "shard", None), P("segment", "shard", None), P("segment"))
    out_specs = (
        P("segment", "shard", None),
        P("segment", "shard", None),
        P("segment", "shard", None),
    )
    return jax.shard_map(body, mesh=mesh, in_specs=in_specs, out_specs=out_specs, check_vma=False)
```

profile of v0, /device:TPU:0, one launch (start us, length us, event | category | flops | bytes accessed | tf_op | source)
XLA Modules:
  0.0 498.2 jit_solution(15562166234760625701)
XLA Ops:
  7.2 0.0 all-gather.2.cloned.1.call-start
  7.2 0.7 all-gather.2.cloned.1.call-update
  7.9 0.0 all-reduce.5.cloned.1.call-start
  7.9 56.8 %all-gather.2.cloned.1.call-done = bf16[2,2304,256]{2,1,0:T(8,128)(2,1)} async-done(((bf16[2,288,256]{2,1,0:T(8,128)(2,1)}), bf16[2,2304,256]{2,1,0:T(8,128)(2,1)}) %all-gather.2.cloned.1.call-update) | async-done | bytes 2359312 | tf_op jit(solution)/shard_map/all_gather | solution.py:59
  64.7 10.6 %fusion.20 = f32[2,2304,256]{2,1,0:T(8,128)S(1)} fusion(bf16[2,2304,2304]{2,1,0:T(8,128)(2,1)} %param.3, bf16[2,2304,256]{2,1,0:T(8,128)(2,1)} %all-gather.2.cloned.1.call-done), kind=kOutput, calls=%fused_computation.47 | convolution fusion | flops 5435817984 | bytes 28311552 | tf_op jit(solution)/shard_map/kij,kjr->kir/dot_general | solution.py:56
  75.4 0.0 copy-start
  75.4 2.2 copy-done
  77.6 8.4 %fusion.21 = f32[2,256,256]{1,2,0:T(8,128)} fusion(f32[2,2304,256]{2,1,0:T(8,128)S(1)} %fusion.20), kind=kOutput, calls=%fused_computation.48 | convolution fusion | flops 3623878656 | bytes 5242880 | tf_op jit(solution)/shard_map/kir,kis->krs/dot_general | solution.py:62
  86.0 0.0 all-reduce.5.cloned.1.call-update
  86.0 0.5 all-reduce.7.cloned.1.call-start
  86.6 70.8 %all-reduce.5.cloned.1.call-done = f32[2,256,256]{1,2,0:T(8,128)} async-done(((f32[2,256,256]{1,2,0:T(8,128)}), f32[2,256,256]{1,2,0:T(8,128)}) %all-reduce.5.cloned.1.call-update) | async-done | bytes 524304 | tf_op jit(solution)/shard_map/psum | solution.py:63
  157.4 1.2 copy.22
  158.7 1.1 fusion.9
  159.8 23.5 %custom-call.17 = f32[2,128,128]{2,1,0:T(8,128)S(1)} custom-call(f32[2,128,128]{2,1,0:T(8,128)S(1)} %cholesky.122), custom_call_target="Cholesky" | custom-call | tf_op jit(solution)/shard_map/jit(cholesky)/cholesky | solution.py:13
  183.3 19.7 %custom-call.18 = f32[2,1,128,128]{2,3,1,0:T(8,128)S(1)} custom-call(f32[2,1,128,128]{3,2,1,0:T(8,128)S(1)} %select_bitcast_fusion), custom_call_target="InvertDiagBlocksLowerTriangular" | custom-call | tf_op jit(solution)/shard_map/jit(cholesky)/cholesky | solution.py:13
  203.0 0.3 constant_dynamic-update-slice_fusion.1
  203.3 0.4 convolution_subtract_fusion.1
  203.7 23.5 %custom-call.19 = f32[2,128,128]{2,1,0:T(8,128)S(1)} custom-call(f32[2,128,128]{2,1,0:T(8,128)S(1)} %convolution_subtract_fusion.1), custom_call_target="Cholesky" | custom-call | tf_op jit(solution)/shard_map/jit(cholesky)/cholesky | solution.py:13
  227.2 0.2 compare_reduce_fusion
  227.3 0.1 select_select_fusion
  227.5 0.1 triangular_solve.62
  227.6 4.1 while.1
  227.6 0.6 fusion.32
  228.2 1.4 bitcast_dynamic-update-slice_fusion.2
  229.6 0.6 fusion.32
  230.2 1.4 bitcast_dynamic-update-slice_fusion.2
  231.7 39.5 %custom-call.20 = f32[2,2,128,128]{2,3,1,0:T(8,128)S(1)} custom-call(f32[2,2,128,128]{3,2,1,0:T(8,128)S(1)} %bitcast.52), custom_call_target="InvertDiagBlocksLowerTriangular" | custom-call | tf_op jit(solution)/shard_map/jit(_solve_triangular)/vmap()/triangular_solve | solution.py:14
  271.2 0.0 copy-start.1
  271.2 4.0 fusion.5
  275.2 0.0 copy-done.1
  275.2 3.9 convolution_subtract_fusion
  279.1 2.2 fusion.13
  281.3 0.0 copy-start.2
  281.4 1.4 copy-done.2
  282.8 12.2 %convolution_bitcast_fusion = f32[2,2304,256]{1,2,0:T(8,128)} fusion(bf16[2,2304,2304]{2,1,0:T(8,128)(2,1)} %param.3, f32[2,128,2304]{2,1,0:T(8,128)S(1)} %fusion.13, f32[2,128,2304]{2,1,0:T(8,128)S(1)} %fusion.5), kind=kOutput, calls=%fused_computation.7 | convolution fusion | flops 5440536576 | bytes 30670848 | tf_op jit(solution)/shard_map/kij,kir->kjr/dot_general | solution.py:32
  295.0 0.0 all-reduce.7.cloned.1.call-update
  295.7 13.7 %fusion.2 = f32[2]{0:T(128)S(1)} fusion(bf16[2,2304,2304]{2,1,0:T(8,128)(2,1)} %param.3), kind=kLoop, calls=%fused_computation.6 | loop fusion | flops 31850494 | bytes 21233672 | tf_op jit(solution)/shard_map/reduce_sum | solution.py:51
  309.4 0.6 select_reduce_fusion.2
  310.0 43.1 %all-reduce.1 = (f32[]{:T(128)}, f32[]{:T(128)}) all-reduce(f32[]{:T(128)} %select_reduce_fusion.2, f32[]{:T(128)S(6)} %mul.46), channel_id=1, replica_groups=mesh['segment'=4,'shard'=8] {'segment','shard'}, use_global_device_ids=true, to_apply=%region_8.9 | all-reduce | flops 2 | bytes 16 | tf_op jit(solution)/shard_map/psum | solution.py:54
  354.5 3.6 fusion.4
  358.1 4.3 copy.32
  362.4 102.5 %all-reduce.7.cloned.1.call-done = f32[2,2304,256]{1,2,0:T(8,128)} async-done(((f32[2,2304,256]{1,2,0:T(8,128)}), f32[2,2304,256]{1,2,0:T(8,128)}) %all-reduce.7.cloned.1.call-update) | async-done | bytes 4718608 | tf_op jit(solution)/shard_map/psum | solution.py:22
  464.9 2.7 multiply_reduce_fusion
  467.6 1.6 fusion.8
  469.2 1.1 copy.33
  470.3 21.2 %fusion.1 = bf16[2,2304,2304]{2,1,0:T(8,128)(2,1)} fusion(bf16[2,2304,2304]{2,1,0:T(8,128)(2,1)} %param.3, pred[2]{0:T(512)(128)(4,1)S(1)} %iota_compare_fusion.3, f32[2,2304,256]{1,2,0:T(8,128)} %all-reduce.7.cloned.1.call-done, f32[2,128,2304]{2,1,0:T(8,128)} %copy-done.2, f32[2,128,2304]{2,1,0:T(8,128)S(1)} %fusion.5), kind=kOutput, calls=%fused_computation.5 | convolution fusion | flops 5494800384 | bytes 51904512 | tf_op jit(solution)/shard_map/kir,kjr->kij/dot_general | solution.py:34
  (14 shorter events, 0.2 us)
Async XLA Ops:
  7.2 57.6 %all-gather.2.cloned.1.call-start = ((), (), s32[]{:S(2)}) async-start(), calls=%async_computation | async-start | bytes 2654208 | tf_op jit(solution)/shard_map/all_gather | solution.py:59
  7.9 149.5 %all-reduce.5.cloned.1.call-start = ((), (), s32[]{:S(2)}) async-start(), calls=%async_computation.1 | async-start | bytes 1048576 | tf_op jit(solution)/shard_map/psum | solution.py:63
  75.4 2.2 copy-start
  86.0 378.9 %all-reduce.7.cloned.1.call-start = ((), (), s32[]{:S(2)}) async-start(), calls=%async_computation.2 | async-start | bytes 9437184 | tf_op jit(solution)/shard_map/psum | solution.py:22
  271.2 4.0 copy-start.1
  281.3 1.4 copy-start.2
Sparse Core Ops, SparseCore 0:
  10.2 54.5 all-gather.1
  86.1 71.2 all-reduce.4
  295.2 169.6 all-reduce.6
where the time goes:
time: 506 us; the launch traced here: 498 us
  waiting for transfers between devices  231 us (46%)
  other arithmetic  130 us (26%)
  matrix products  63.2 us (12%)
  blocking collectives  43.1 us (9%)
  between operations  16.2 us (3%)
  local copies, waits for them, and re-layouts  14.4 us (3%)
    psum x1, waiting for transfers between devices, right_factor(): full = lax.psum(partial_value, 'shard')  102 us
    psum x1, waiting for transfers between devices, body(): gram = lax.psum(local_gram, 'shard')  70.8 us
    another operation x9, other arithmetic, finish_basis(): lower = jnp.linalg.cholesky(gram)  66.8 us
    all_gather x1, waiting for transfers between devices, body(): lax.all_gather(right_basis, 'shard', axis=1, tiled=True)  56.8 us
    psum x1, blocking collectives, body(): lax.psum((local_sq, local_elems), ('segment', 'shard'))  43.1 us
    another operation x4, other arithmetic, finish_basis(): jax.scipy.linalg.solve_triangular(lower, jnp.swapaxes(proj, 1, 2), lower=...  39.7 us
    dot_general x1, matrix products, finish_layers(): jnp.einsum('kir,kjr->kij', half_left, half_right, preferred_element_type=...  21.2 us
    reduce_sum x1, other arithmetic, body(): per_slot = jnp.sum(jnp.square(buffer.astype(jnp.float32)), axis=(1, 2))  13.7 us
  transfers between devices with their start and end apart: 3, of which 3 were waited for; matrix products, arithmetic and copies ran while one was open for 4% of the time, Pallas kernels for 0%

commit v1 on v0

--- a/solution.py
+++ b/solution.py
@@ -60,7 +60,11 @@
         preferred_element_type=jnp.float32,
     )
     local_gram = jnp.einsum("kir,kis->krs", proj, proj, precision=lax.Precision.HIGHEST)
-    gram = lax.psum(local_gram, "shard")
+
+    def draft_sums_all(sheet, which_axis):
+        return jnp.sum(lax.all_gather(sheet, axis_name=which_axis), axis=0)
+
+    gram = draft_sums_all(local_gram, "shard")
     return finish_layers(buffer, proj, gram, used, clip, rows_all)
 
 

time: 506 us -> 507 us (level)
    all_gather x0 -> x1, waiting for transfers between devices: none -> 70.9 us  [draft_sums_all(): return jnp.sum(lax.all_gather(sheet, axis_name=which_axis), axis=0)]
    psum x1 -> x0, waiting for transfers between devices: 70.8 us -> none  [body(): gram = lax.psum(local_gram, 'shard')]
where the time goes in v1:
time: 507 us; the launch traced here: 500 us
  waiting for transfers between devices  231 us (46%)
  other arithmetic  131 us (26%)
  matrix products  64.7 us (13%)
  blocking collectives  42.6 us (8%)
  between operations  16.2 us (3%)
  local copies, waits for them, and re-layouts  13.4 us (3%)
    psum x1, waiting for transfers between devices, right_factor(): full = lax.psum(partial_value, 'shard')  102 us
    all_gather x1, waiting for transfers between devices, draft_sums_all(): return jnp.sum(lax.all_gather(sheet, axis_name=which_axis), axis=0)  70.9 us
    another operation x9, other arithmetic, finish_basis(): lower = jnp.linalg.cholesky(gram)  66.8 us
    all_gather x1, waiting for transfers between devices, body(): lax.all_gather(right_basis, 'shard', axis=1, tiled=True)  56.8 us
    psum x1, blocking collectives, body(): lax.psum((local_sq, local_elems), ('segment', 'shard'))  42.6 us
    another operation x4, other arithmetic, finish_basis(): jax.scipy.linalg.solve_triangular(lower, jnp.swapaxes(proj, 1, 2), lower=...  39.7 us
    dot_general x1, matrix products, finish_layers(): jnp.einsum('kir,kjr->kij', half_left, half_right, preferred_element_type=...  21.2 us
    reduce_sum x1, other arithmetic, body(): per_slot = jnp.sum(jnp.square(buffer.astype(jnp.float32)), axis=(1, 2))  13.7 us
  transfers between devices with their start and end apart: 3, of which 3 were waited for; matrix products, arithmetic and copies ran while one was open for 4% of the time, Pallas kernels for 0%

profile of v1, /device:TPU:0, one launch (start us, length us, event | category | flops | bytes accessed | tf_op | source)
XLA Modules:
  0.0 499.5 jit_solution(9257963927521960486)
XLA Ops:
  7.2 0.0 all-gather.4.cloned.1.call-start
  7.2 0.7 all-gather.4.cloned.1.call-update
  7.9 0.0 all-gather.6.cloned.1.call-start
  7.9 56.8 %all-gather.4.cloned.1.call-done = bf16[2,2304,256]{2,1,0:T(8,128)(2,1)} async-done(((bf16[2,288,256]{2,1,0:T(8,128)(2,1)}), bf16[2,2304,256]{2,1,0:T(8,128)(2,1)}) %all-gather.4.cloned.1.call-update) | async-done | bytes 2359312 | tf_op jit(solution)/shard_map/all_gather | solution.py:59
  64.7 10.6 %fusion.20 = f32[2,2304,256]{2,1,0:T(8,128)S(1)} fusion(bf16[2,2304,2304]{2,1,0:T(8,128)(2,1)} %param.3, bf16[2,2304,256]{2,1,0:T(8,128)(2,1)} %all-gather.4.cloned.1.call-done), kind=kOutput, calls=%fused_computation.47 | convolution fusion | flops 5435817984 | bytes 28311552 | tf_op jit(solution)/shard_map/kij,kjr->kir/dot_general | solution.py:56
  75.4 0.0 copy-start
  75.4 2.2 copy-done
  77.6 8.4 %fusion.21 = f32[2,256,256]{2,1,0:T(8,128)} fusion(f32[2,2304,256]{2,1,0:T(8,128)S(1)} %fusion.20), kind=kOutput, calls=%fused_computation.48 | convolution fusion | flops 3623878656 | bytes 5242880 | tf_op jit(solution)/shard_map/kir,kis->krs/dot_general | solution.py:62
  86.0 0.0 all-gather.6.cloned.1.call-update
  86.0 0.5 all-reduce.4.cloned.1.call-start
  86.7 70.9 %all-gather.6.cloned.1.call-done = f32[16,256,256]{2,1,0:T(8,128)} async-done(((f32[2,256,256]{2,1,0:T(8,128)}), f32[16,256,256]{2,1,0:T(8,128)}) %all-gather.6.cloned.1.call-update) | async-done | bytes 4194320 | tf_op jit(solution)/shard_map/all_gather | solution.py:65
  157.5 2.5 reduce_sum.36
  160.0 0.2 copy.33
  160.2 0.1 fusion.9
  160.3 23.5 %custom-call.17 = f32[2,128,128]{2,1,0:T(8,128)S(1)} custom-call(f32[2,128,128]{2,1,0:T(8,128)S(1)} %cholesky.122), custom_call_target="Cholesky" | custom-call | tf_op jit(solution)/shard_map/jit(cholesky)/cholesky | solution.py:13
  183.9 19.7 %custom-call.18 = f32[2,1,128,128]{2,3,1,0:T(8,128)S(1)} custom-call(f32[2,1,128,128]{3,2,1,0:T(8,128)S(1)} %select_bitcast_fusion), custom_call_target="InvertDiagBlocksLowerTriangular" | custom-call | tf_op jit(solution)/shard_map/jit(cholesky)/cholesky | solution.py:13
  203.5 0.3 constant_dynamic-update-slice_fusion.1
  203.8 0.4 convolution_subtract_fusion.1
  204.2 23.5 %custom-call.19 = f32[2,128,128]{2,1,0:T(8,128)S(1)} custom-call(f32[2,128,128]{2,1,0:T(8,128)S(1)} %convolution_subtract_fusion.1), custom_call_target="Cholesky" | custom-call | tf_op jit(solution)/shard_map/jit(cholesky)/cholesky | solution.py:13
  227.7 0.2 compare_reduce_fusion
  227.9 0.1 select_select_fusion
  228.0 0.1 triangular_solve.62
  228.1 4.1 while.1
  228.1 0.6 fusion.32
  228.7 1.4 bitcast_dynamic-update-slice_fusion.2
  230.2 0.6 fusion.32
  230.8 1.4 bitcast_dynamic-update-slice_fusion.2
  232.2 39.5 %custom-call.20 = f32[2,2,128,128]{2,3,1,0:T(8,128)S(1)} custom-call(f32[2,2,128,128]{3,2,1,0:T(8,128)S(1)} %bitcast.54), custom_call_target="InvertDiagBlocksLowerTriangular" | custom-call | tf_op jit(solution)/shard_map/jit(_solve_triangular)/vmap()/triangular_solve | solution.py:14
  271.7 3.8 fusion.5
  275.6 5.6 %convolution_subtract_fusion = f32[2,128,2304]{1,2,0:T(8,128)S(1)} fusion(f32[2,128,2304]{2,1,0:T(8,128)S(1)} %fusion.5, f32[2,256,2304]{1,2,0:T(8,128)} %bitcast.52, f32[2,256,256]{2,1,0:T(8,128)S(1)} %get-tuple-element.90), kind=kOutput, calls=%fused_computation.11 | convolution fusion | flops 906559488 | bytes 7208960 | tf_op jit(solution)/shard_map/jit(_solve_triangular)/vmap()/triangular_solve | solution.py:14
  281.1 2.2 fusion.13
  283.4 0.0 copy-start.1
  283.4 1.4 copy-done.1
  284.8 12.2 %convolution_bitcast_fusion = f32[2,2304,256]{1,2,0:T(8,128)} fusion(bf16[2,2304,2304]{2,1,0:T(8,128)(2,1)} %param.3, f32[2,128,2304]{2,1,0:T(8,128)S(1)} %fusion.13, f32[2,128,2304]{2,1,0:T(8,128)S(1)} %fusion.5), kind=kOutput, calls=%fused_computation.7 | convolution fusion | flops 5440536576 | bytes 30670848 | tf_op jit(solution)/shard_map/kij,kir->kjr/dot_general | solution.py:32
  297.1 0.0 all-reduce.4.cloned.1.call-update
  297.7 13.7 %fusion.2 = f32[2]{0:T(128)S(1)} fusion(bf16[2,2304,2304]{2,1,0:T(8,128)(2,1)} %param.3), kind=kLoop, calls=%fused_computation.6 | loop fusion | flops 31850494 | bytes 21233672 | tf_op jit(solution)/shard_map/reduce_sum | solution.py:51
  311.4 0.6 select_reduce_fusion.2
  312.0 42.6 %all-reduce.1 = (f32[]{:T(128)}, f32[]{:T(128)}) all-reduce(f32[]{:T(128)} %select_reduce_fusion.2, f32[]{:T(128)S(6)} %mul.46), channel_id=1, replica_groups=mesh['segment'=4,'shard'=8] {'segment','shard'}, use_global_device_ids=true, to_apply=%region_8.9 | all-reduce | flops 2 | bytes 16 | tf_op jit(solution)/shard_map/psum | solution.py:54
  356.0 3.6 fusion.4
  359.6 4.3 copy.44
  363.9 102.3 %all-reduce.4.cloned.1.call-done = f32[2,2304,256]{1,2,0:T(8,128)} async-done(((f32[2,2304,256]{1,2,0:T(8,128)}), f32[2,2304,256]{1,2,0:T(8,128)}) %all-reduce.4.cloned.1.call-update) | async-done | bytes 4718608 | tf_op jit(solution)/shard_map/psum | solution.py:22
  466.2 2.7 multiply_reduce_fusion
  468.9 1.6 fusion.8
  470.5 1.1 copy.45
  471.6 21.2 %fusion.1 = bf16[2,2304,2304]{2,1,0:T(8,128)(2,1)} fusion(bf16[2,2304,2304]{2,1,0:T(8,128)(2,1)} %param.3, pred[2]{0:T(512)(128)(4,1)S(1)} %iota_compare_fusion.3, f32[2,2304,256]{1,2,0:T(8,128)} %all-reduce.4.cloned.1.call-done, f32[2,128,2304]{2,1,0:T(8,128)} %copy-done.1, f32[2,128,2304]{2,1,0:T(8,128)S(1)} %fusion.5), kind=kOutput, calls=%fused_computation.5 | convolution fusion | flops 5494800384 | bytes 51904512 | tf_op jit(solution)/shard_map/kir,kjr->kij/dot_general | solution.py:34
  (14 shorter events, 0.2 us)
Async XLA Ops:
  7.2 57.6 %all-gather.4.cloned.1.call-start = ((), (), s32[]{:S(2)}) async-start(), calls=%async_computation | async-start | bytes 2654208 | tf_op jit(solution)/shard_map/all_gather | solution.py:59
  7.9 149.6 %all-gather.6.cloned.1.call-start = ((), (), s32[]{:S(2)}) async-start(), calls=%async_computation.2 | async-start | bytes 4718592 | tf_op jit(solution)/shard_map/all_gather | solution.py:65
  75.4 2.2 copy-start
  86.0 380.2 %all-reduce.4.cloned.1.call-start = ((), (), s32[]{:S(2)}) async-start(), calls=%async_computation.1 | async-start | bytes 9437184 | tf_op jit(solution)/shard_map/psum | solution.py:22
  283.4 1.4 copy-start.1
Sparse Core Ops, SparseCore 0:
  10.2 54.5 all-gather.3
  86.2 71.3 all-gather.5
  297.2 168.9 all-reduce.3
